TPU v7x, 256 devices: a whole 4x4x8 slice. The times are simulated.
256 devices in a mesh: dp: 64 (over z, y, core), mp: 4 (over x).
Axes of the slice: x: 4, y: 4, z: 8, core: 2. Of those that a mesh axis runs over, the one named last changes fastest.
Arguments:
- tokens: bfloat16 [393216, 512], P('dp'), may hold values from -6 to 6
- w_uvqk: bfloat16 [512, 2048], P(None, 'mp')
- w_out: bfloat16 [512, 512], replicated, may hold values from -0.25 to 0.25
- hist_len: int32 [64, 24], P('dp'), may hold values from 64 to 256, as said below
- owner: int32 [64, 24], P('dp'), may hold values from 0 to 63, as said below
- recv_offset: int32 [64, 24], P('dp'), may hold values from 0 to 47, as said below
- block_start: int32 [64, 24], P('dp'), may hold values from 0 to 47, as said below
Outputs:
- packed_out: bfloat16 [393216, 512], P('dp', 'mp')
- user_state: bfloat16 [1536, 512], P('dp', 'mp')
Inputs may be any that keep to these rules, and one draw needn't show every extreme that they name: User (d, u) has ceil(hist_len / 128) blocks, at most 2. owner[d, u] = (p(d) + r(u mod 64)) mod 64 for two permutations p, r of the indices of dp drawn from the seed: every owner receives exactly 24 users, and one device sends at most 1 users to one owner. On some owner every received user has 2 blocks. `recv_offset`: the users of one owner occupy disjoint runs of its 48 blocks, in the order of u; on some owner they fill all 48 blocks. `block_start`: the users of one device occupy disjoint runs of its 48 blocks, in the order of u.
All inputs are finite; a program needn't handle non-finite values.
Results may differ from a plain program's by a relative error of at most 0.0059.
Values may be sent and summed in bfloat16 or wider, within the bound.
A program may use at most 128 MiB of HBM per device.

v0:
```python
import jax
import jax.numpy as jnp
from jax import lax
from jax.sharding import PartitionSpec as P

D = 512
HEADS = 4
BLOCK = 128
MAXB = 2
BLK_DEV = 48
EPS = 1e-05


def sent_to_all(shard, axis):
    count = lax.axis_size(axis)
    return lax.all_to_all(
        jnp.broadcast_to(shard[None], (count, *shard.shape)), axis, 0, 0, tiled=True
    )


def over_copies(shard, axis):
    everything = sent_to_all(shard, axis)
    return jnp.sum(everything, axis=0)


def together(arrays, axis):
    ends = [0]
    for a in arrays:
        ends.append(ends[-1] + a.size)
    subtotal = over_copies(jnp.concatenate([a.ravel() for a in arrays]), axis)
    return tuple((subtotal[b:e].reshape(a.shape) for a, b, e in zip(arrays, ends, ends[1:])))


def in_one_piece(arrays, axis, dim, along):
    widths = [a.shape[along] for a in arrays]
    both = jnp.concatenate(arrays, axis=along)
    result = lax.all_gather(both, axis, axis=dim, tiled=True)
    return tuple(jnp.split(result, [sum(widths[:k]) for k in range(1, len(widths))], axis=along))


def norm_rows(values):
    average = jnp.mean(values, axis=-1, keepdims=True)
    variance = jnp.mean(values * values, axis=-1, keepdims=True) - average * average
    return (values - average) * lax.rsqrt(variance + EPS)


def attend(query, keys, values, query_user, key_user):
    row_count, head_size = query.shape
    tile_rows = 4 * BLOCK
    back_rows = (MAXB - 1) * BLOCK
    scaling = (D // HEADS) ** (-0.5)
    keys_ext = jnp.concatenate([jnp.zeros((back_rows, head_size), keys.dtype), keys], 0)
    values_ext = jnp.concatenate([jnp.zeros((back_rows, head_size), values.dtype), values], 0)
    users_ext = jnp.concatenate([jnp.full((back_rows,), -2, jnp.int32), key_user], 0)
    query_pos = jnp.arange(tile_rows, dtype=jnp.int32)[:, None] + back_rows
    key_pos = jnp.arange(tile_rows + back_rows, dtype=jnp.int32)[None, :]

    def one_tile(start):
        query_tile = lax.dynamic_slice_in_dim(query, start, tile_rows, 0)
        key_tile = lax.dynamic_slice_in_dim(keys_ext, start, tile_rows + back_rows, 0)
        value_tile = lax.dynamic_slice_in_dim(values_ext, start, tile_rows + back_rows, 0)
        query_owner = lax.dynamic_slice_in_dim(query_user, start, tile_rows, 0)
        key_owner = lax.dynamic_slice_in_dim(users_ext, start, tile_rows + back_rows, 0)
        raw_scores = (
            lax.dot_general(
                query_tile, key_tile, (((1,), (1,)), ((), ())), preferred_element_type=jnp.float32
            )
            * scaling
        )
        allowed = (query_owner[:, None] == key_owner[None, :]) & (key_pos <= query_pos)
        weights = jnp.where(allowed, jax.nn.silu(raw_scores) / (MAXB * BLOCK), 0.0).astype(
            jnp.bfloat16
        )
        return jnp.dot(weights, value_tile, preferred_element_type=jnp.float32)

    tile_starts = jnp.arange(row_count // tile_rows, dtype=jnp.int32) * tile_rows
    return lax.map(one_tile, tile_starts).reshape(row_count, head_size)


def layer_rows(rows_in, query_user, key_user, w_uvqk, w_out):
    row_count = rows_in.shape[0]
    head_size = D // HEADS
    mp_size = lax.axis_size("mp")
    portion = lax.axis_index("mp")
    quarter = D // mp_size
    local_heads = w_uvqk.shape[1] // (4 * head_size)
    widened = rows_in.astype(jnp.float32)
    normed = norm_rows(widened).astype(jnp.bfloat16)
    projected = jax.nn.silu(jnp.dot(normed, w_uvqk, preferred_element_type=jnp.float32)).astype(
        jnp.bfloat16
    )
    pieces = projected.reshape(row_count, local_heads, 4, head_size)
    outputs = attend(pieces[:, 0, 2], pieces[:, 0, 3], pieces[:, 0, 1], query_user, key_user)
    totals = together((jnp.sum(outputs, 1), jnp.sum(outputs * outputs, 1)), "mp")
    average = totals[0] / D
    variance = totals[1] / D - average * average
    gates = pieces[:, :, 0].reshape(row_count, local_heads * head_size).astype(jnp.float32)
    gated_rows = ((outputs - average[:, None]) * lax.rsqrt(variance + EPS)[:, None] * gates).astype(
        jnp.bfloat16
    )
    every_head = lax.all_gather(gated_rows, "mp", axis=1, tiled=True)
    out_columns = lax.dynamic_slice_in_dim(w_out, portion * quarter, quarter, 1)
    mixed_rows = jnp.dot(every_head, out_columns, preferred_element_type=jnp.float32)
    residual = lax.dynamic_slice_in_dim(widened, portion * quarter, quarter, 1)
    return (mixed_rows + residual).astype(jnp.bfloat16)


def row_labels(block_user, block_fill):
    in_block = jnp.arange(BLOCK, dtype=jnp.int32)[None, :]
    row_live = (in_block < block_fill[:, None]).reshape(-1)
    row_user = jnp.broadcast_to(block_user[:, None], (block_user.shape[0], BLOCK)).reshape(-1)
    return (row_live, jnp.where(row_live, row_user, -3), jnp.where(row_live, row_user, -2))


def per_device(tokens, w_uvqk, w_out, hist_len, owner, recv_offset, block_start):
    dp_size = lax.axis_size("dp")
    mp_size = lax.axis_size("mp")
    myself = lax.axis_index("dp")
    user_count = hist_len.shape[1]
    per_pair = -(-user_count // dp_size)
    pair_cap = per_pair * MAXB
    quarter = D // mp_size
    lengths = hist_len[0]
    owners = owner[0]
    starts = block_start[0]
    counts = (lengths + BLOCK - 1) // BLOCK
    user_ids = jnp.arange(user_count, dtype=jnp.int32)
    earlier = user_ids[None, :] < user_ids[:, None]
    same_owner = (owners[:, None] == owners[None, :]) & earlier
    in_pair = jnp.sum(jnp.where(same_owner, counts[None, :], 0), axis=1)
    slot_ids = jnp.arange(pair_cap, dtype=jnp.int32)
    device_ids = jnp.arange(dp_size, dtype=jnp.int32)
    slot_step = slot_ids[None, :, None] - in_pair[None, None, :]
    sending = (
        (owners[None, None, :] == device_ids[:, None, None])
        & (slot_step >= 0)
        & (slot_step < counts[None, None, :])
    )
    send_block = jnp.sum(jnp.where(sending, starts[None, None, :] + slot_step, 0), axis=2)
    all_len, all_owner, all_offset = in_one_piece((hist_len, owner, recv_offset), "dp", 0, 1)
    all_counts = (all_len + BLOCK - 1) // BLOCK
    all_before = (all_owner[:, :, None] == all_owner[:, None, :]) & earlier[None]
    all_in_pair = jnp.sum(jnp.where(all_before, all_counts[:, None, :], 0), axis=2)
    owned = all_owner == myself
    flat_owned = owned.reshape(-1)
    flat_len = all_len.reshape(-1)
    flat_offset = all_offset.reshape(-1)
    flat_counts = all_counts.reshape(-1)
    flat_in_pair = all_in_pair.reshape(-1)
    candidate_ids = jnp.arange(dp_size * user_count, dtype=jnp.int32)
    source_ids = candidate_ids // user_count
    block_ids = jnp.arange(BLK_DEV, dtype=jnp.int32)
    land_step = block_ids[:, None] - flat_offset[None, :]
    landed = flat_owned[None, :] & (land_step >= 0) & (land_step < flat_counts[None, :])
    slot_index = jnp.sum(
        jnp.where(landed, source_ids[None, :] * pair_cap + flat_in_pair[None, :] + land_step, 0),
        axis=1,
    )
    owned_user = jnp.sum(jnp.where(landed, candidate_ids[None, :], 0), axis=1)
    owned_fill = jnp.sum(
        jnp.where(landed, jnp.clip(flat_len[None, :] - land_step * BLOCK, 0, BLOCK), 0), axis=1
    )
    owned_live, owned_query, owned_key = row_labels(owned_user, owned_fill)
    local_step = block_ids[:, None] - starts[None, :]
    within = (local_step >= 0) & (local_step < counts[None, :])
    local_user = jnp.sum(jnp.where(within, user_ids[None, :], 0), axis=1)
    local_fill = jnp.sum(
        jnp.where(within, jnp.clip(lengths[None, :] - local_step * BLOCK, 0, BLOCK), 0), axis=1
    )
    local_live, local_query, local_key = row_labels(local_user, local_fill)
    results = layer_rows(tokens, local_query, local_key, w_uvqk, w_out)
    state = jnp.take(results, starts * BLOCK + lengths - 1, axis=0)
    outgoing = jnp.take(results.reshape(BLK_DEV, BLOCK, quarter), send_block, axis=0)
    arrived = lax.all_to_all(outgoing, "dp", split_axis=0, concat_axis=0, tiled=True)
    gathered = jnp.take(
        arrived.reshape(dp_size * pair_cap, BLOCK, quarter), slot_index, axis=0
    ).reshape(BLK_DEV * BLOCK, quarter)
    packed = jnp.where(owned_live[:, None], gathered, jnp.zeros_like(gathered))
    return (packed, state)


def solution(mesh):
    in_specs = (
        P("dp", None),
        P(None, "mp"),
        P(),
        P("dp", None),
        P("dp", None),
        P("dp", None),
        P("dp", None),
    )
    out_specs = (P("dp", "mp"), P("dp", "mp"))
    return jax.shard_map(
        per_device, mesh=mesh, in_specs=in_specs, out_specs=out_specs, check_vma=False
    )
```

profile of v0, /device:TPU:1, one launch (start us, length us, event | category | flops | bytes accessed | tf_op | source)
XLA Modules:
  0.0 370.8 jit_solution(17628559279992237693)
XLA Ops:
  7.2 4.8 %convert_reduce_fusion = (f32[6144]{0:T(1024)S(1)}, f32[6144]{0:T(1024)S(1)}) fusion(bf16[6144,512]{1,0:T(8,128)(2,1)} %param.9), kind=kLoop, calls=%fused_computation.31 | loop fusion | flops 12570624 | bytes 6340608 | tf_op jit(solution)/shard_map/reduce_sum | solution.py:42
  12.0 8.0 %multiply_convert_fusion = bf16[6144,512]{0,1:T(8,128)(2,1)S(1)} fusion(bf16[512,512]{1,0:T(8,128)(2,1)S(1)} %copy-done, bf16[6144,512]{1,0:T(8,128)(2,1)S(1)} %copy-done.2, f32[6144]{0:T(1024)S(1)} %get-tuple-element.108, f32[6144]{0:T(1024)S(1)} %get-tuple-element.107), kind=kOutput, calls=%fused_computation.28 | convolution fusion | flops 3249537024 | bytes 13156352 | tf_op jit(solution)/shard_map/dot_general | solution.py:89
  20.0 2.3 fusion.59
  22.3 1.3 copy-done.3
  23.7 2.6 copy.50
  26.3 2.6 copy.51
  28.9 2.8 concatenate.17
  31.7 1.3 concatenate.18
  33.0 1.6 copy.49
  34.7 78.6 %while.11 = (s32[]{:T(128)}, f32[12,512,128]{2,1,0:T(8,128)}, s32[12]{0:T(128)S(1)}, s32[6144]{0:T(1024)S(1)}, s32[6272]{0:T(1024)S(1)}, /*index=5*/bf16[6144,12...) while((s32[]{:T(128)}, f32[12,512,128]{2,1,0:T(8,128)}, ...), condition=%wide.region_10.11_spmd.clone, body=%wide.region_9.10_spmd.clone.sunk | while | flops 171377152 | bytes 741060 | solution.py:77
  34.8 0.6 dynamic_slice.53
  38.7 2.6 fusion.70
  41.3 0.6 dynamic_slice.53
  45.3 2.6 fusion.70
  47.9 0.6 dynamic_slice.53
  51.8 2.6 fusion.70
  54.4 0.6 dynamic_slice.53
  58.4 2.6 fusion.70
  61.0 0.6 dynamic_slice.53
  64.9 2.6 fusion.70
  67.5 0.6 dynamic_slice.53
  71.5 2.6 fusion.70
  74.1 0.6 dynamic_slice.53
  78.0 2.6 fusion.70
  80.6 0.6 dynamic_slice.53
  84.5 2.6 fusion.70
  87.2 0.6 dynamic_slice.53
  91.1 2.6 fusion.70
  93.7 0.6 dynamic_slice.53
  97.7 2.6 fusion.70
  104.2 2.6 fusion.70
  110.8 2.6 fusion.70
  113.4 3.6 fusion.58
  117.0 0.8 broadcast_in_dim.174
  117.8 4.8 %all-to-all-start = ((f32[4,1,12288]{2,1,0:T(1,128)}), f32[4,1,12288]{2,1,0:T(1,128)S(1)}, u32[]{:S(2)}, u32[]{:S(2)}) async-start(f32[4,1,12288]{2,1,0:T(1,128)} %broadcast_in_dim.174), calls=%async_computation | async-start | bytes 393216 | tf_op jit(solution)/shard_map/all_to_all | solution.py:16
  122.6 3.5 copy.46
  126.2 1.6 all-to-all-done
  128.0 4.0 %fusion.30 = bf16[6144,128]{0,1:T(8,128)(2,1)} fusion(f32[6144,128]{0,1:T(8,128)} %copy.46, bf16[6144,1,4,128]{0,3,2,1:T(8,128)(2,1)} %bitcast.68, f32[6144]{0:T(1024)S(1)} %get-tuple-element.102, f32[6144]{0:T(1024)S(1)} %get-tuple-element.101), kind=kLoop, calls=%fused_computation.39 | loop fusion | flops 3932160 | bytes 6340608 | tf_op jit(solution)/shard_map/convert_element_type | solution.py:98
  132.0 9.2 %convert_element_type.24 = f32[6144,512]{1,0:T(8,128)} convert(bf16[6144,512]{1,0:T(8,128)(2,1)} %param.9) | non-fusion elementwise | flops 3145728 | bytes 18874368 | tf_op jit(solution)/shard_map/convert_element_type | solution.py:87
  142.0 60.7 %all-gather.3.cloned.1.call-done = bf16[6144,512]{0,1:T(8,128)(2,1)} async-done(((bf16[6144,128]{0,1:T(8,128)(2,1)}), bf16[6144,512]{0,1:T(8,128)(2,1)}) %all-gather.3.cloned.1.call-update) | async-done | bytes 6291472 | tf_op jit(solution)/shard_map/all_gather | solution.py:101
  202.7 5.6 %fusion.26 = bf16[6144,128]{1,0:T(8,128)(2,1)S(1)} fusion(bf16[6144,512]{0,1:T(8,128)(2,1)} %all-gather.3.cloned.1.call-done, f32[6144,512]{1,0:T(8,128)} %convert_element_type.24, s32[]{:T(128)S(6)} %select_n.164, bf16[512,512]{1,0:T(8,128)(2,1)} %param.11), kind=kOutput, calls=%fused_computation.33 | convolution fusion | flops 806879232 | bytes 11142144 | tf_op jit(solution)/shard_map/dot_general | solution.py:103
  208.4 3.1 gather_fusion
  211.4 4.6 %broadcast_select_fusion = bf16[64,2,128,128]{3,2,1,0:T(8,128)(2,1)} fusion(bf16[64,2,128,128]{3,2,1,0:T(8,128)(2,1)} %bitcast.65, pred[64,2]{1,0:T(8,128)(4,1)S(1)} %copy.41), kind=kLoop, calls=%fused_computation.37 | loop fusion | flops 2097152 | bytes 8388736 | tf_op jit(solution)/shard_map/jit(_take)/select_n | solution.py:173
  216.0 11.2 %all-to-all-start.1 = ((bf16[64,2,128,128]{3,2,1,0:T(8,128)(2,1)}), bf16[64,2,128,128]{3,2,1,0:T(8,128)(2,1)}, u32[]{:S(2)}, u32[]{:S(2)}) async-start(bf16[64,2,128,128]{3,2,1,0:T(8,128)(2,1)} %broadcast_select_fusion), calls=%async_computation.1 | async-start | bytes 8388608 | tf_op jit(solution)/shard_map/all_to_all | solution.py:174
  227.3 125.6 %all-gather = s32[64,1,72]{2,1,0:T(1,128)S(1)} all-gather(s32[1,1,72]{2,1,0:T(1,128)S(1)} %add_bitcast_fusion), channel_id=1, replica_groups=mesh['dp'=64,'mp'=4] {'dp'}, dimensions={0}, use_global_device_ids=true | all-gather | bytes 18720 | tf_op jit(solution)/shard_map/all_gather | solution.py:37
  355.0 0.7 broadcast_select_fusion.1
  355.6 3.1 gather_fusion.1
  358.7 5.2 %fusion.31 = bf16[6144,128]{1,0:T(8,128)(2,1)} fusion(bf16[48,128,128]{2,1,0:T(8,128)(2,1)S(1)} %gather_fusion.1, pred[6144]{0:T(1024)(128)(4,1)S(1)} %get-tuple-element.114, pred[6144]{0:T(1024)(128)(4,1)S(1)} %get-tuple-element.113), kind=kLoop, calls=%fused_computation.43 | loop fusion | flops 1572864 | bytes 3158016 | tf_op jit(solution)/shard_map/jit(_where)/select_n | solution.py:178
  (105 shorter events, 6.5 us)
Async XLA Ops:
  7.2 4.8 %copy-start = (bf16[512,512]{1,0:T(8,128)(2,1)S(1)}, bf16[512,512]{1,0:T(8,128)(2,1)}, u32[]{:S(2)}) copy-start(bf16[512,512]{1,0:T(8,128)(2,1)} %param.10) | copy-start | bytes 1572868
  7.2 4.8 %copy-start.2 = (bf16[6144,512]{1,0:T(8,128)(2,1)S(1)}, bf16[6144,512]{1,0:T(8,128)(2,1)}, u32[]{:S(2)}) copy-start(bf16[6144,512]{1,0:T(8,128)(2,1)} %param.9) | copy-start | bytes 18874372
  20.0 3.7 copy-start.3
  28.9 2.8 copy-start.4
  31.7 2.8 copy-start.6
  31.7 2.8 copy-start.7
  117.8 10.0 %all-to-all-start = ((f32[4,1,12288]{2,1,0:T(1,128)}), f32[4,1,12288]{2,1,0:T(1,128)S(1)}, u32[]{:S(2)}, u32[]{:S(2)}) async-start(f32[4,1,12288]{2,1,0:T(1,128)} %broadcast_in_dim.174), calls=%async_computation | async-start | bytes 393216 | tf_op jit(solution)/shard_map/all_to_all | solution.py:16
  122.6 80.1 %all-gather.3.cloned.1.call-start = ((), (), s32[]{:S(2)}) async-start(), calls=%async_computation.2 | async-start | bytes 7864320 | tf_op jit(solution)/shard_map/all_gather | solution.py:101
  132.0 9.2 %copy-start.5 = (s32[1,24]{1,0:T(1,128)S(1)}, s32[1,24]{1,0:T(1,128)}, u32[]{:S(2)}) copy-start(s32[1,24]{1,0:T(1,128)} %param.13) | copy-start | bytes 292
  216.0 11.2 %copy-start.8 = (s32[1,24]{1,0:T(1,128)S(1)}, s32[1,24]{1,0:T(1,128)}, u32[]{:S(2)}) copy-start(s32[1,24]{1,0:T(1,128)} %param.14) | copy-start | bytes 292
  216.0 139.6 %all-to-all-start.1 = ((bf16[64,2,128,128]{3,2,1,0:T(8,128)(2,1)}), bf16[64,2,128,128]{3,2,1,0:T(8,128)(2,1)}, u32[]{:S(2)}, u32[]{:S(2)}) async-start(bf16[64,2,128,128]{3,2,1,0:T(8,128)(2,1)} %broadcast_select_fusion), calls=%async_computation.1 | async-start | bytes 8388608 | tf_op jit(solution)/shard_map/all_to_all | solution.py:174
  355.6 8.3 %copy-start.1 = (bf16[512,512]{1,0:T(8,128)(2,1)S(1)}, bf16[512,512]{1,0:T(8,128)(2,1)}, u32[]{:S(2)}) copy-start(bf16[512,512]{1,0:T(8,128)(2,1)} %param.10) | copy-start | bytes 1572868
Sparse Core Ops, SparseCore 0:
  132.1 70.5 all-gather.2
where the time goes:
time: 372 us; the launch traced here: 371 us
  blocking collectives  126 us (34%)
  waiting for transfers between devices  62.4 us (17%)
  matrix products  45 us (12%)
  loops' own time  37.9 us (10%)
  local copies, waits for them, and re-layouts  35.9 us (10%)
  other arithmetic  33.7 us (9%)
  starting transfers between devices  16 us (4%)
  between operations  14.3 us (4%)
    all_gather x1, blocking collectives, in_one_piece(): result = lax.all_gather(both, axis, axis=dim, tiled=True)  126 us
    all_gather x1, waiting for transfers between devices, layer_rows(): every_head = lax.all_gather(gated_rows, 'mp', axis=1, tiled=True)  60.7 us
    another operation x1, loops' own time, attend(): return lax.map(one_tile, tile_starts).reshape(row_count, head_size)  37.9 us
    dot_general x12, matrix products, one_tile(): return jnp.dot(weights, value_tile, preferred_element_type=jnp.float32)  31.4 us
    all_to_all x1, starting transfers between devices, per_device(): lax.all_to_all(outgoing, 'dp', split_axis=0, concat_axis=0, tiled=True)  11.2 us
    convert_element_type x1, other arithmetic, layer_rows(): widened = rows_in.astype(jnp.float32)  9.17 us
    unnamed x21, local copies, waits for them, and re-layouts  8.13 us
    dot_general x1, matrix products, layer_rows(): jnp.dot(normed, w_uvqk, preferred_element_type=jnp.float32)  7.98 us
  transfers between devices with their start and end apart: 3, of which 2 were waited for; matrix products, arithmetic and copies ran while one was open for 4% of the time, Pallas kernels for 0%

commit v1 on v0

--- a/solution.py
+++ b/solution.py
@@ -98,7 +98,9 @@
     gated_rows = ((outputs - average[:, None]) * lax.rsqrt(variance + EPS)[:, None] * gates).astype(
         jnp.bfloat16
     )
-    every_head = lax.all_gather(gated_rows, "mp", axis=1, tiled=True)
+    every_head = jnp.concatenate(
+        lax.all_to_all(jnp.stack([gated_rows] * lax.axis_size("mp")), "mp", 0, 0), axis=1
+    )
     out_columns = lax.dynamic_slice_in_dim(w_out, portion * quarter, quarter, 1)
     mixed_rows = jnp.dot(every_head, out_columns, preferred_element_type=jnp.float32)
     residual = lax.dynamic_slice_in_dim(widened, portion * quarter, quarter, 1)

time: 372 us -> 369 us (level)
  between operations: 14.3 us -> 0.96 us
  starting transfers between devices: 16 us -> 26 us
    all_gather x1 -> x0, waiting for transfers between devices: 60.7 us -> none  [layer_rows(): every_head = lax.all_gather(gated_rows, 'mp', axis=1, tiled=True)]
    all_to_all x0 -> x1, waiting for transfers between devices: none -> 58.4 us  [layer_rows(): lax.all_to_all(jnp.stack([gated_rows] * lax.axis_size('mp')), 'mp', 0, 0)]
    all_to_all x0 -> x1, starting transfers between devices: none -> 5.46 us  [layer_rows(): lax.all_to_all(jnp.stack([gated_rows] * lax.axis_size('mp')), 'mp', 0, 0)]
    all_to_all x1, starting transfers between devices: 11.2 us -> 15.7 us  [per_device(): lax.all_to_all(outgoing, 'dp', split_axis=0, concat_axis=0, tiled=True)]
where the time goes in v1:
time: 369 us; the launch traced here: 367 us
  blocking collectives  126 us (34%)
  waiting for transfers between devices  60.1 us (16%)
  matrix products  45 us (12%)
  local copies, waits for them, and re-layouts  39.3 us (11%)
  loops' own time  37.9 us (10%)
  other arithmetic  32.5 us (9%)
  starting transfers between devices  26 us (7%)
    all_gather x1, blocking collectives, in_one_piece(): result = lax.all_gather(both, axis, axis=dim, tiled=True)  126 us
    all_to_all x1, waiting for transfers between devices, layer_rows(): lax.all_to_all(jnp.stack([gated_rows] * lax.axis_size('mp')), 'mp', 0, 0)  58.4 us
    another operation x1, loops' own time, attend(): return lax.map(one_tile, tile_starts).reshape(row_count, head_size)  37.9 us
    dot_general x12, matrix products, one_tile(): return jnp.dot(weights, value_tile, preferred_element_type=jnp.float32)  31.4 us
    all_to_all x1, starting transfers between devices, per_device(): lax.all_to_all(outgoing, 'dp', split_axis=0, concat_axis=0, tiled=True)  15.7 us
    convert_element_type x1, other arithmetic, layer_rows(): widened = rows_in.astype(jnp.float32)  9.17 us
    unnamed x21, local copies, waits for them, and re-layouts  8.14 us
    dot_general x1, matrix products, layer_rows(): jnp.dot(normed, w_uvqk, preferred_element_type=jnp.float32)  7.98 us
  transfers between devices with their start and end apart: 3, of which 2 were waited for; matrix products, arithmetic and copies ran while one was open for 4% of the time, Pallas kernels for 0%

profile of v1, /device:TPU:1, one launch (start us, length us, event | category | flops | bytes accessed | tf_op | source)
XLA Modules:
  0.0 367.4 jit_solution(1588174501374040545)
XLA Ops:
  0.7 4.8 %convert_reduce_fusion = (f32[6144]{0:T(1024)S(1)}, f32[6144]{0:T(1024)S(1)}) fusion(bf16[6144,512]{1,0:T(8,128)(2,1)} %param.9), kind=kLoop, calls=%fused_computation.31 | loop fusion | flops 12570624 | bytes 6340608 | tf_op jit(solution)/shard_map/reduce_sum | solution.py:42
  5.5 8.0 %multiply_convert_fusion = bf16[6144,512]{0,1:T(8,128)(2,1)S(1)} fusion(bf16[512,512]{1,0:T(8,128)(2,1)S(1)} %copy-done, bf16[6144,512]{1,0:T(8,128)(2,1)S(1)} %copy-done.2, f32[6144]{0:T(1024)S(1)} %get-tuple-element.108, f32[6144]{0:T(1024)S(1)} %get-tuple-element.107), kind=kOutput, calls=%fused_computation.28 | convolution fusion | flops 3249537024 | bytes 13156352 | tf_op jit(solution)/shard_map/dot_general | solution.py:89
  13.5 2.3 fusion.59
  15.8 1.3 copy-done.3
  17.1 2.6 copy.51
  19.7 2.6 copy.52
  22.3 2.8 concatenate.17
  25.1 1.3 concatenate.18
  26.4 1.6 copy.50
  28.2 78.6 %while.11 = (s32[]{:T(128)}, f32[12,512,128]{2,1,0:T(8,128)}, s32[12]{0:T(128)S(1)}, s32[6144]{0:T(1024)S(1)}, s32[6272]{0:T(1024)S(1)}, /*index=5*/bf16[6144,12...) while((s32[]{:T(128)}, f32[12,512,128]{2,1,0:T(8,128)}, ...), condition=%wide.region_10.11_spmd.clone, body=%wide.region_9.10_spmd.clone.sunk | while | flops 171377152 | bytes 741060 | solution.py:77
  28.2 0.6 dynamic_slice.53
  32.1 2.6 fusion.70
  34.7 0.6 dynamic_slice.53
  38.7 2.6 fusion.70
  45.2 2.6 fusion.70
  51.8 2.6 fusion.70
  54.4 0.6 dynamic_slice.53
  58.3 2.6 fusion.70
  64.9 2.6 fusion.70
  71.4 2.6 fusion.70
  74.0 0.6 dynamic_slice.53
  78.0 2.6 fusion.70
  80.6 0.6 dynamic_slice.53
  84.5 2.6 fusion.70
  87.1 0.6 dynamic_slice.53
  91.1 2.6 fusion.70
  93.7 0.6 dynamic_slice.53
  97.6 2.6 fusion.70
  100.2 0.6 dynamic_slice.53
  104.2 2.6 fusion.70
  106.8 3.6 fusion.58
  110.4 0.8 broadcast_in_dim.174
  111.2 4.8 %all-to-all-start = ((f32[4,1,12288]{2,1,0:T(1,128)}), f32[4,1,12288]{2,1,0:T(1,128)S(1)}, u32[]{:S(2)}, u32[]{:S(2)}) async-start(f32[4,1,12288]{2,1,0:T(1,128)} %broadcast_in_dim.174), calls=%async_computation | async-start | bytes 393216 | tf_op jit(solution)/shard_map/all_to_all | solution.py:16
  116.0 3.5 copy.47
  119.6 1.6 all-to-all-done
  121.4 2.8 fusion.30
  124.3 3.5 stack.2
  127.8 5.5 %all-to-all-start.1 = ((bf16[4,6144,128]{1,2,0:T(8,128)(2,1)}), bf16[4,6144,128]{1,2,0:T(8,128)(2,1)}, u32[]{:S(2)}, u32[]{:S(2)}) async-start(bf16[4,6144,128]{1,2,0:T(8,128)(2,1)} %stack.2), calls=%async_computation.1 | async-start | bytes 12582912 | tf_op jit(solution)/shard_map/all_to_all | solution.py:102
  133.2 9.2 %convert_element_type.28 = f32[6144,512]{1,0:T(8,128)} convert(bf16[6144,512]{1,0:T(8,128)(2,1)} %param.9) | non-fusion elementwise | flops 3145728 | bytes 18874368 | tf_op jit(solution)/shard_map/convert_element_type | solution.py:87
  143.2 58.4 %all-to-all-done.1 = bf16[4,6144,128]{1,2,0:T(8,128)(2,1)} async-done(((bf16[4,6144,128]{1,2,0:T(8,128)(2,1)}), bf16[4,6144,128]{1,2,0:T(8,128)(2,1)}, u32[]{:S(2)}, u32[]{:S(2)}) %all-to-all-start.1) | async-done | bytes 6291488 | tf_op jit(solution)/shard_map/all_to_all | solution.py:102
  201.6 5.6 %fusion.26 = bf16[6144,128]{1,0:T(8,128)(2,1)S(1)} fusion(bf16[6144,512]{0,1:T(8,128)(2,1)} %bitcast.17, f32[6144,512]{1,0:T(8,128)} %convert_element_type.28, s32[]{:T(128)S(6)} %select_n.164, bf16[512,512]{1,0:T(8,128)(2,1)} %param.11), kind=kOutput, calls=%fused_computation.33 | convolution fusion | flops 806879232 | bytes 11142144 | tf_op jit(solution)/shard_map/dot_general | solution.py:105
  207.3 3.1 gather_fusion
  210.3 4.6 %broadcast_select_fusion = bf16[64,2,128,128]{3,2,1,0:T(8,128)(2,1)} fusion(bf16[64,2,128,128]{3,2,1,0:T(8,128)(2,1)} %bitcast.68, pred[64,2]{1,0:T(8,128)(4,1)S(1)} %copy.42), kind=kLoop, calls=%fused_computation.37 | loop fusion | flops 2097152 | bytes 8388736 | tf_op jit(solution)/shard_map/jit(_take)/select_n | solution.py:175
  214.9 15.7 %all-to-all-start.2 = ((bf16[64,2,128,128]{3,2,1,0:T(8,128)(2,1)}), bf16[64,2,128,128]{3,2,1,0:T(8,128)(2,1)}, u32[]{:S(2)}, u32[]{:S(2)}) async-start(bf16[64,2,128,128]{3,2,1,0:T(8,128)(2,1)} %broadcast_select_fusion), calls=%async_computation.2 | async-start | bytes 8388608 | tf_op jit(solution)/shard_map/all_to_all | solution.py:176
  230.7 125.6 %all-gather = s32[64,1,72]{2,1,0:T(1,128)S(1)} all-gather(s32[1,1,72]{2,1,0:T(1,128)S(1)} %add_bitcast_fusion), channel_id=1, replica_groups=mesh['dp'=64,'mp'=4] {'dp'}, dimensions={0}, use_global_device_ids=true | all-gather | bytes 18720 | tf_op jit(solution)/shard_map/all_gather | solution.py:37
  358.4 0.7 broadcast_select_fusion.1
  359.1 3.1 gather_fusion.1
  362.2 5.2 %fusion.31 = bf16[6144,128]{1,0:T(8,128)(2,1)} fusion(bf16[48,128,128]{2,1,0:T(8,128)(2,1)S(1)} %gather_fusion.1, pred[6144]{0:T(1024)(128)(4,1)S(1)} %get-tuple-element.114, pred[6144]{0:T(1024)(128)(4,1)S(1)} %get-tuple-element.113), kind=kLoop, calls=%fused_computation.43 | loop fusion | flops 1572864 | bytes 3158016 | tf_op jit(solution)/shard_map/jit(_where)/select_n | solution.py:180
  (105 shorter events, 7.7 us)
Async XLA Ops:
  0.6 4.8 %copy-start = (bf16[512,512]{1,0:T(8,128)(2,1)S(1)}, bf16[512,512]{1,0:T(8,128)(2,1)}, u32[]{:S(2)}) copy-start(bf16[512,512]{1,0:T(8,128)(2,1)} %param.10) | copy-start | bytes 1572868
  0.7 4.8 %copy-start.2 = (bf16[6144,512]{1,0:T(8,128)(2,1)S(1)}, bf16[6144,512]{1,0:T(8,128)(2,1)}, u32[]{:S(2)}) copy-start(bf16[6144,512]{1,0:T(8,128)(2,1)} %param.9) | copy-start | bytes 18874372
  13.5 3.6 copy-start.3
  22.3 2.8 copy-start.4
  25.1 2.8 copy-start.6
  25.1 2.8 copy-start.7
  111.2 10.0 %all-to-all-start = ((f32[4,1,12288]{2,1,0:T(1,128)}), f32[4,1,12288]{2,1,0:T(1,128)S(1)}, u32[]{:S(2)}, u32[]{:S(2)}) async-start(f32[4,1,12288]{2,1,0:T(1,128)} %broadcast_in_dim.174), calls=%async_computation | async-start | bytes 393216 | tf_op jit(solution)/shard_map/all_to_all | solution.py:16
  127.8 73.9 %all-to-all-start.1 = ((bf16[4,6144,128]{1,2,0:T(8,128)(2,1)}), bf16[4,6144,128]{1,2,0:T(8,128)(2,1)}, u32[]{:S(2)}, u32[]{:S(2)}) async-start(bf16[4,6144,128]{1,2,0:T(8,128)(2,1)} %stack.2), calls=%async_computation.1 | async-start | bytes 12582912 | tf_op jit(solution)/shard_map/all_to_all | solution.py:102
  133.2 9.2 %copy-start.5 = (s32[1,24]{1,0:T(1,128)S(1)}, s32[1,24]{1,0:T(1,128)}, u32[]{:S(2)}) copy-start(s32[1,24]{1,0:T(1,128)} %param.13) | copy-start | bytes 292
  214.9 15.7 %copy-start.8 = (s32[1,24]{1,0:T(1,128)S(1)}, s32[1,24]{1,0:T(1,128)}, u32[]{:S(2)}) copy-start(s32[1,24]{1,0:T(1,128)} %param.14) | copy-start | bytes 292
  214.9 144.2 %all-to-all-start.2 = ((bf16[64,2,128,128]{3,2,1,0:T(8,128)(2,1)}), bf16[64,2,128,128]{3,2,1,0:T(8,128)(2,1)}, u32[]{:S(2)}, u32[]{:S(2)}) async-start(bf16[64,2,128,128]{3,2,1,0:T(8,128)(2,1)} %broadcast_select_fusion), calls=%async_computation.2 | async-start | bytes 8388608 | tf_op jit(solution)/shard_map/all_to_all | solution.py:176
  359.0 8.3 %copy-start.1 = (bf16[512,512]{1,0:T(8,128)(2,1)S(1)}, bf16[512,512]{1,0:T(8,128)(2,1)}, u32[]{:S(2)}) copy-start(bf16[512,512]{1,0:T(8,128)(2,1)} %param.10) | copy-start | bytes 1572868
